TPU v7x, 32 devices: a whole 2x2x4 slice. The times are simulated.
32 devices in a mesh: groups: 2 (over x), blk: 4 (over y, core), col: 4 (over z).
Axes of the slice: x: 2, y: 2, z: 4, core: 2. Of those that a mesh axis runs over, the one named last changes fastest.
Arguments:
- pair_block: bfloat16 [4096, 16384], P(('groups', 'blk'), 'col'), parts along dimension 0, may hold values from -1.5 to 1.5
- occ_energy: float32 [2], P('groups'), parts along dimension 0, may hold values from -1.5 to -0.3
- virt_energy: float32 [4096], P('groups'), parts along dimension 0, may hold values from 0.2 to 3
- frequency: float32 [2], P('groups'), parts along dimension 0, may hold values from 0.2 to 2
Outputs:
- dielectric: float32 [32768, 16384], P(('groups', 'col'), 'blk'), parts along dimension 0
There are 2 independent parts, one for each index of `groups`. A program takes and returns all parts, laid end to end along the dimension named above; each array names one. Nothing has to cross between parts.
All inputs are finite; a program needn't handle non-finite values.
Results may differ from a plain program's by a relative error of at most 0.0027.
Values may be sent and summed in bfloat16 or wider, within the bound.
A program may use at most 192 MiB of HBM per device.

v0:
```python
import jax
import jax.numpy as jnp
from jax import lax
from jax.sharding import PartitionSpec as P


def pair_weights(occ_energy, virt_energy, frequency):
    gap = (virt_energy[None, :] - occ_energy[:, None]).reshape(-1)
    return 2.0 * gap / (gap * gap + frequency[0] * frequency[0])


def shards(pair_block, occ_energy, virt_energy, frequency):
    weights = pair_weights(occ_energy, virt_energy, frequency)
    row_full = lax.all_gather(pair_block, "col", axis=1, tiled=True)
    column_slab = lax.all_to_all(row_full, "blk", split_axis=1, concat_axis=0, tiled=True)
    scaled = (
        lax.all_gather(pair_block, "blk", axis=0, tiled=True).astype(jnp.float32) * weights[:, None]
    ).astype(jnp.bfloat16)
    return lax.dot_general(
        scaled, column_slab, (((0,), (0,)), ((), ())), preferred_element_type=jnp.float32
    )


def solution(mesh):
    return jax.shard_map(
        shards,
        mesh=mesh,
        in_specs=(P(("groups", "blk"), "col"), P("groups"), P("groups"), P("groups")),
        out_specs=P(("groups", "col"), "blk"),
        check_vma=False,
    )
```

profile of v0, /device:TPU:16, one launch (start us, length us, event | category | flops | bytes accessed | tf_op | source)
XLA Modules:
  0.0 687.8 jit_solution(8358652491445676149)
XLA Ops:
  6.5 0.0 all-gather.5.cloned.1.call-start
  6.5 6.4 copy.5
  12.9 0.0 all-gather.5.cloned.1.call-update
  13.0 0.0 all-gather.3.cloned.1.call-start
  13.0 0.7 all-gather.3.cloned.1.call-update
  13.7 285.4 %all-gather.5.cloned.1.call-done = bf16[512,16384]{0,1:T(8,128)(2,1)} async-done(((bf16[512,4096]{0,1:T(8,128)(2,1)}), bf16[512,16384]{0,1:T(8,128)(2,1)}) %all-gather.5.cloned.1.call-update) | async-done | bytes 16777232 | tf_op jit(solution)/shard_map/all_gather | solution.py:14
  299.1 0.0 copy-start
  299.1 7.1 %all-to-all-start = ((bf16[512,4,4096]{0,2,1:T(8,128)(2,1)}), bf16[512,4,4096]{0,2,1:T(8,128)(2,1)}, u32[]{:S(2)}, u32[]{:S(2)}) async-start(bf16[512,4,4096]{0,2,1:T(8,128)(2,1)} %bitcast.8), calls=%async_computation | async-start | bytes 33554432 | tf_op jit(solution)/shard_map/all_to_all | solution.py:15
  307.6 0.0 copy-done
  307.6 271.6 %all-to-all-done = bf16[512,4,4096]{0,2,1:T(8,128)(2,1)} async-done(((bf16[512,4,4096]{0,2,1:T(8,128)(2,1)}), bf16[512,4,4096]{0,2,1:T(8,128)(2,1)}, u32[]{:S(2)}, u32[]{:S(2)}) %all-to-all-start) | async-done | bytes 16777248 | tf_op jit(solution)/shard_map/all_to_all | solution.py:15
  579.2 20.7 %copy.6 = bf16[4,512,4096]{2,1,0:T(8,128)(2,1)} copy(bf16[4,512,4096]{1,2,0:T(8,128)(2,1)} %bitcast.3) | data formatting | bytes 33554432 | tf_op jit(solution)/shard_map/all_to_all | solution.py:15
  599.8 0.0 all-gather.3.cloned.1.call-done
  599.8 81.2 %fusion = f32[4096,4096]{1,0:T(8,128)} fusion(bf16[2048,4096]{1,0:T(8,128)(2,1)} %bitcast.9, bf16[2048,4096]{1,0:T(8,128)(2,1)} %all-gather.3.cloned.1.call-done, f32[2048]{0:T(1024)S(1)} %add_divide_fusion), kind=kOutput, calls=%fused_computation.1 | convolution fusion | flops 68744642560 | bytes 100671488 | tf_op jit(solution)/shard_map/dot_general | solution.py:19
  (1 shorter events, 0.0 us)
Async XLA Ops:
  6.5 292.6 %all-gather.5.cloned.1.call-start = ((), (), s32[]{:S(2)}) async-start(), calls=%async_computation.2 | async-start | bytes 20971520 | tf_op jit(solution)/shard_map/all_gather | solution.py:14
  13.0 586.9 %all-gather.3.cloned.1.call-start = ((), (), s32[]{:S(2)}) async-start(), calls=%async_computation.1 | async-start | bytes 20971520 | tf_op jit(solution)/shard_map/all_gather | solution.py:17
  299.1 8.4 %copy-start = (f32[2048]{0:T(1024)S(1)}, f32[2048]{0:T(1024)}, u32[]{:S(2)}) copy-start(f32[2048]{0:T(1024)} %param.6) | copy-start | bytes 24580
  299.1 280.0 %all-to-all-start = ((bf16[512,4,4096]{0,2,1:T(8,128)(2,1)}), bf16[512,4,4096]{0,2,1:T(8,128)(2,1)}, u32[]{:S(2)}, u32[]{:S(2)}) async-start(bf16[512,4,4096]{0,2,1:T(8,128)(2,1)} %bitcast.8), calls=%async_computation | async-start | bytes 33554432 | tf_op jit(solution)/shard_map/all_to_all | solution.py:15
Sparse Core Ops, SparseCore 0:
  13.1 286.0 all-gather.4
  300.7 195.8 all-gather.2
where the time goes:
time: 692 us; the launch traced here: 688 us
  waiting for transfers between devices  558 us (81%)
  matrix products  81.2 us (12%)
  local copies, waits for them, and re-layouts  27.1 us (4%)
  between operations  14.7 us (2%)
  starting transfers between devices  7.14 us (1%)
    all_gather x1, waiting for transfers between devices, shards(): row_full = lax.all_gather(pair_block, 'col', axis=1, tiled=True)  285 us
    all_to_all x1, waiting for transfers between devices, shards(): lax.all_to_all(row_full, 'blk', split_axis=1, concat_axis=0, tiled=True)  272 us
    dot_general x1, matrix products, shards(): lax.dot_general(scaled, column_slab, (((0,), (0,)), ((), ())), preferred_...  81.2 us
    all_to_all x1, local copies, waits for them, and re-layouts, shards(): lax.all_to_all(row_full, 'blk', split_axis=1, concat_axis=0, tiled=True)  20.7 us
  transfers between devices with their start and end apart: 3, of which 2 were waited for; matrix products, arithmetic and copies ran while one was open for 3% of the time, Pallas kernels for 0%

commit v1 on v0

v1 whole, which is shorter than its diff:
```python
import functools

import jax
import jax.numpy as jnp
from jax import lax
from jax.experimental import pallas as pl
from jax.experimental.pallas import tpu as pltpu
from jax.sharding import PartitionSpec as P

MESH = pl.DeviceIdType.MESH
CHUNKS = 8
TO_Y, TO_SIB, FWD_SIB, ECHO, PART0, LOCAL0, ON_XB, LINE0, LINE1, CROSS0, CROSS1 = 0, 1, 2, 3, 4, 8, 12, 16, 17, 18, 19


def pair_weights(occ_energy, virt_energy, frequency):
    gap = (virt_energy[None, :] - occ_energy[:, None]).reshape(-1)
    return 2.0 * gap / (gap * gap + frequency[0] * frequency[0])


def gather_kernel(x_ref, xz, xb, tr, send, rz, rb, rt):
    rows = x_ref.shape[0]
    step_rows = rows // CHUNKS
    g, b, z = lax.axis_index("groups"), lax.axis_index("blk"), lax.axis_index("col")
    last = lax.axis_size("col") - 1
    y, k = b // 2, b % 2
    u, v = k + y - 2 * y * k, z + y * (last - 2 * z)
    tu, tv = 1 - u, last - v
    dz = 1 - 2 * y
    own, sib, opp, dia = b, 2 * y + 1 - k, 2 * (1 - y) + k, 2 * (1 - y) + 1 - k
    first = 2 * y + y
    second = 2 * y + 1 - y
    far0, far1 = 2 * (1 - y) + y, 2 * (1 - y) + 1 - y

    def at(ref, slot, j):
        return ref.at[pl.ds(pl.multiple_of(slot * rows + j * step_rows, step_rows), step_rows)]

    def copy(src, dst, ssem, rsem, dev):
        return pltpu.make_async_remote_copy(
            src_ref=src, dst_ref=dst, send_sem=ssem, recv_sem=rsem, device_id=(g, dev[0], dev[1]), device_id_type=MESH
        )

    def to(kind, j, src, ref, rsem, slot, dev, lane=0):
        return copy(src, at(ref, slot, j), send.at[kind + lane, j], rsem.at[slot, j], dev)

    def arrived(ref, rsem, slot, j):
        copy(at(ref, slot, j), at(ref, slot, j), send.at[0, j], rsem.at[slot, j], (sib, z)).wait_recv()

    source = v == u
    feeds_sib = v == 1 - u
    tz = -dz
    to_sib = (sib, z)
    hop1 = (b, z + dz * (1 - 2 * u))
    up = (b, z + dz)
    down = (b, z - dz)
    line = (b, z + tz)
    cross0, cross1 = (2 * (1 - y) + 1 - y, z), (2 * (1 - y) + y, z)

    def spread(j, src, shard, lane):
        yield source, to(PART0, j, src, xb, rb, shard, hop1, lane)
        yield feeds_sib, to(LOCAL0, j, src, xb, rb, shard, to_sib, lane)
        if lane < 2:
            yield (u == 1) & (v == 1), to(ON_XB, j, src, xb, rb, shard, up, lane)

    def own_sends(j):
        src = x_ref.at[pl.ds(pl.multiple_of(j * step_rows, step_rows), step_rows)]
        yield True, to(TO_SIB, j, src, xz, rz, own, to_sib)
        yield True, to(TO_Y, j, src, xz, rz, own, (opp, z))
        yield tv == 0, to(LINE0, j, src, tr, rt, 0, line)
        yield tv == 1, to(LINE1, j, src, tr, rt, 1, line)
        yield from spread(j, src, own, 0)

    def sib_sends(j):
        src = at(xz, sib, j)
        yield True, to(ECHO, j, src, xz, rz, sib, to_sib)
        yield from spread(j, src, sib, 1)

    def opp_sends(j):
        src = at(xz, opp, j)
        yield True, to(FWD_SIB, j, src, xz, rz, opp, to_sib)
        yield from spread(j, src, opp, 2)

    def dia_sends(j):
        yield from spread(j, at(xz, dia, j), dia, 3)

    passes = [
        (1, (tv == 1), tr, rt, 0, lambda j: to(LINE0, j, at(tr, 0, j), tr, rt, 0, line)),
        (1, (u == 0) & (v == 1), xb, rb, first, lambda j: to(ON_XB, j, at(xb, first, j), xb, rb, first, up, 0)),
        (2, (u == 1) & (v == 2), xb, rb, second, lambda j: to(ON_XB, j, at(xb, second, j), xb, rb, second, up, 0)),
        (2, (tv == 2), tr, rt, 1, lambda j: to(CROSS1, j, at(tr, 1, j), xb, rb, own, cross1)),
        (3, (u == 0) & (v == 2), xb, rb, first, lambda j: to(ON_XB, j, at(xb, first, j), xb, rb, first, up, 0)),
        (9, (u == 0) & (v == 1), xb, rb, second, lambda j: to(ON_XB, j, at(xb, second, j), xb, rb, second, up, 1)),
        (10, (u == 1) & (v == 2), xb, rb, first, lambda j: to(ON_XB, j, at(xb, first, j), xb, rb, first, up, 1)),
        (10, (tv == 2), tr, rt, 0, lambda j: to(LINE0, j, at(tr, 0, j), tr, rt, 0, line)),
        (11, (tv == 3), tr, rt, 0, lambda j: to(CROSS0, j, at(tr, 0, j), xb, rb, own, cross0)),
        (11, (u == 0) & (v == 2), xb, rb, second, lambda j: to(ON_XB, j, at(xb, second, j), xb, rb, second, up, 1)),
        (11, (u == 1) & (v == 2), xb, rb, far0, lambda j: to(ON_XB, j, at(xb, far0, j), xb, rb, far0, up, 2)),
        (11, (u == 1) & (v == 2), xb, rb, far1, lambda j: to(ON_XB, j, at(xb, far1, j), xb, rb, far1, up, 3)),
        (13, (u == 0) & (v == 3), xb, rb, far0, lambda j: to(ON_XB, j, at(xb, far0, j), xb, rb, far0, down, 2)),
        (13, (u == 0) & (v == 3), xb, rb, far1, lambda j: to(ON_XB, j, at(xb, far1, j), xb, rb, far1, down, 3)),
    ]

    def when(cond, f):
        if cond is True:
            f()
        else:
            pl.when(cond)(f)

    def start_all(sends):
        for cond, c in sends:
            when(cond, c.start)

    barrier = pltpu.get_barrier_semaphore()
    peers = [(sib, z), (opp, z), (dia, z)] + [(b, lax.rem(z + i, last + 1)) for i in range(1, last + 1)]
    for dev in peers:
        pl.semaphore_signal(barrier, inc=1, device_id=(g,) + dev, device_id_type=MESH)
    pl.semaphore_wait(barrier, len(peers))

    @pl.loop(0, CHUNKS)
    def _(j):
        start_all(own_sends(j))

    @pl.loop(0, CHUNKS)
    def _(j):
        arrived(xz, rz, sib, j)
        start_all(sib_sends(j))

    @pl.loop(0, CHUNKS + 13)
    def _(t):
        @pl.when(t < CHUNKS)
        def _():
            arrived(xz, rz, opp, t)
            start_all(opp_sends(t))

        @pl.when((t >= 1) & (t < CHUNKS + 1))
        def _():
            arrived(xz, rz, dia, t - 1)
            start_all(dia_sends(t - 1))

        for lag, role, ref, rsem, slot, send_on in passes:

            @pl.when(role & (t >= lag) & (t < lag + CHUNKS))
            def _():
                arrived(ref, rsem, slot, t - lag)
                send_on(t - lag).start()

    @pl.loop(0, CHUNKS)
    def _(j):
        arrived(xz, rz, own, j)
        near = ((u == 0) & (v == 1)) | (v == 2)
        far = ((u == 1) & (v == 2)) | ((u == 0) & (v == 3))

        @pl.when(jnp.logical_not(near))
        def _():
            arrived(xb, rb, first, j)
            arrived(xb, rb, second, j)

        @pl.when(jnp.logical_not(far))
        def _():
            arrived(xb, rb, far0, j)
            arrived(xb, rb, far1, j)

        for sends in (own_sends(j), sib_sends(j), opp_sends(j), dia_sends(j)):
            for cond, c in sends:
                when(cond, c.wait_send)
        for _, role, _, _, _, send_on in passes:
            pl.when(role)(send_on(j).wait_send)


def gather_both(pair_block):
    rows, cols = pair_block.shape
    full = jax.ShapeDtypeStruct((4 * rows, cols), pair_block.dtype)
    return pl.pallas_call(
        gather_kernel,
        out_shape=(full, full, jax.ShapeDtypeStruct((2 * rows, cols), pair_block.dtype)),
        in_specs=[pl.BlockSpec(memory_space=pl.ANY)],
        out_specs=[pl.BlockSpec(memory_space=pl.ANY)] * 3,
        scratch_shapes=[
            pltpu.SemaphoreType.DMA((20, CHUNKS)),
            pltpu.SemaphoreType.DMA((4, CHUNKS)),
            pltpu.SemaphoreType.DMA((4, CHUNKS)),
            pltpu.SemaphoreType.DMA((2, CHUNKS)),
        ],
        compiler_params=pltpu.CompilerParams(collective_id=0, has_side_effects=True),
    )(pair_block)


def shards(square, pair_block, occ_energy, virt_energy, frequency):
    weights = pair_weights(occ_energy, virt_energy, frequency)
    if square:
        own_columns, column_slab, _ = gather_both(pair_block)
    else:
        row_full = lax.all_gather(pair_block, "col", axis=1, tiled=True)
        column_slab = lax.all_to_all(row_full, "blk", split_axis=1, concat_axis=0, tiled=True)
        own_columns = lax.all_gather(pair_block, "blk", axis=0, tiled=True)
    scaled = (own_columns.astype(jnp.float32) * weights[:, None]).astype(jnp.bfloat16)
    return lax.dot_general(
        scaled, column_slab, (((0,), (0,)), ((), ())), preferred_element_type=jnp.float32
    )


def solution(mesh):
    square = mesh.shape["blk"] == 4 and mesh.shape["col"] == 4
    return jax.shard_map(
        functools.partial(shards, square),
        mesh=mesh,
        in_specs=(P(("groups", "blk"), "col"), P("groups"), P("groups"), P("groups")),
        out_specs=P(("groups", "col"), "blk"),
        check_vma=False,
    )
```

time: 692 us -> 422 us (0.61)
  waiting for transfers between devices: 558 us -> 0 us
  Pallas kernels: 0 us -> 339 us
  local copies, waits for them, and re-layouts: 27.1 us -> 0 us
  between operations: 14.7 us -> 1.31 us
  starting transfers between devices: 7.14 us -> 0 us
    pallas_call x0 -> x1, Pallas kernels: none -> 339 us  [gather_both(): pl.pallas_call(gather_kernel, out_shape=(full, full, jax.ShapeDtypeStruct...]
    all_gather x2 -> x0, waiting for transfers between devices: 285 us -> none  [the longest x1 285 us: shards(): row_full = lax.all_gather(pair_block, 'col', axis=1, tiled=True)]
    all_to_all x1 -> x0, waiting for transfers between devices: 272 us -> none  [shards(): lax.all_to_all(row_full, 'blk', split_axis=1, concat_axis=0, tiled=True)]
    all_to_all x1 -> x0, local copies, waits for them, and re-layouts: 20.7 us -> none  [shards(): lax.all_to_all(row_full, 'blk', split_axis=1, concat_axis=0, tiled=True)]
    all_to_all x1 -> x0, starting transfers between devices: 7.1 us -> none  [shards(): lax.all_to_all(row_full, 'blk', split_axis=1, concat_axis=0, tiled=True)]
  transfers between devices with their start and end apart: 3 -> 0, of which waited for: 2 -> 0; matrix products, arithmetic and copies ran while one was open for 3% -> 0% of each run, Pallas kernels for 0% -> 0%
where the time goes in v1:
time: 422 us
  Pallas kernels  339 us (80%)
  matrix products  81.1 us (19%)
    pallas_call x1, Pallas kernels, gather_both(): pl.pallas_call(gather_kernel, out_shape=(full, full, jax.ShapeDtypeStruct...  339 us
    dot_general x1, matrix products, shards(): lax.dot_general(scaled, column_slab, (((0,), (0,)), ((), ())), preferred_...  81.1 us

profile of v1, /device:TPU:16, one launch (start us, length us, event | category | flops | bytes accessed | tf_op | source)
XLA Modules:
  0.0 421.9 jit_solution(9831215618635554082)
XLA Ops:
  1.3 0.7 add_divide_fusion
  2.0 338.7 %shard_map.46 = (bf16[2048,4096]{1,0:T(8,128)(2,1)}, bf16[2048,4096]{1,0:T(8,128)(2,1)}, bf16[1024,4096]{1,0:T(8,128)(2,1)}) custom-call(bf16[512,4096]{1,0:T(8,128)(2,1)} %x_ref.1), custom_call_target="tpu_custom_call" | custom-call | tf_op jit(solution)/shard_map/pallas_call | solution.py:172
  340.7 81.1 %fusion = f32[4096,4096]{1,0:T(8,128)} fusion(bf16[2048,4096]{1,0:T(8,128)(2,1)} %get-tuple-element.8, bf16[2048,4096]{1,0:T(8,128)(2,1)} %get-tuple-element.7, f32[2048]{0:T(1024)S(1)} %add_divide_fusion), kind=kOutput, calls=%fused_computation.1 | convolution fusion | flops 68744642560 | bytes 100671488 | tf_op jit(solution)/shard_map/dot_general | solution.py:196
